TPU v7x, 64 devices: a 2x2x8 block of a 4x4x8 slice. The times are simulated.
64 devices in a mesh: rep: 8 (over x, y, core), dp: 8 (over z).
Axes of the slice: x: 2, y: 2, z: 8, core: 2. Of those that a mesh axis runs over, the one named last changes fastest.
The devices are a block of a 4x4x8 slice.
Arguments:
- a: bfloat16 [64, 4, 4096, 768], P(('rep', 'dp')), parts along dimension 0
- g: bfloat16 [64, 4, 4096, 2048], P(('rep', 'dp')), parts along dimension 0
Outputs:
- output: bfloat16 [32, 768, 2048], P('rep'), parts along dimension 0
There are 8 independent parts. A program takes and returns all parts, laid end to end along the dimension named above; each array names one.
All inputs are finite; a program needn't handle non-finite values.
Results may differ from a plain program's by a relative error of at most 0.012.
Values are sent between devices in bfloat16 or wider.
A program may use at most 768 MiB of HBM per device.

v0:
```python
import jax
import jax.numpy as jnp


def solution(mesh):
    groups = mesh.shape["rep"]

    def step(a, g):
        a, g = (t.reshape(groups, -1, *t.shape[1:]) for t in (a, g))
        sums = jnp.einsum("rsntd,rsntf->rndf", a, g, preferred_element_type=jnp.float32)
        return sums.astype(jnp.bfloat16).reshape(-1, *sums.shape[2:])

    return step
```

profile of v0, /device:TPU:21, one launch (start us, length us, event | category | flops | bytes accessed | tf_op | source)
XLA Modules:
  0.0 555.9 jit_solution(9880827563703156499)
XLA Ops:
  0.0 61.1 %fusion.3 = f32[1,4,768,2048]{3,2,1,0:T(8,128)} fusion(bf16[1,4,4096,2048]{3,2,1,0:T(8,128)(2,1)} %param.1, bf16[1,4,4096,768]{3,2,1,0:T(8,128)(2,1)} %param), kind=kOutput, calls=%fused_computation.4 | convolution fusion | flops 51539607552 | bytes 117440512 | tf_op jit(solution)/rsntd,rsntf->rndf/dot_general | solution.py:10
  61.1 494.9 %all-reduce.2 = bf16[1,4,768,2048]{3,2,1,0:T(8,128)(2,1)} all-reduce(f32[1,4,768,2048]{3,2,1,0:T(8,128)} %fusion.3), channel_id=1, replica_groups=[8,8]<=[64], use_global_device_ids=true, to_apply=%add.clone | all-reduce | flops 6291456 | bytes 37748736 | tf_op jit(solution)/rsntd,rsntf->rndf/dot_general | solution.py:10
where the time goes:
time: 557 us; the launch traced here: 556 us
  blocking collectives  495 us (89%)
  matrix products  61.1 us (11%)
    dot_general x1, blocking collectives, step(): jnp.einsum('rsntd,rsntf->rndf', a, g, preferred_element_type=jnp.float32)  495 us
    dot_general x1, matrix products, step(): jnp.einsum('rsntd,rsntf->rndf', a, g, preferred_element_type=jnp.float32)  61.1 us

commit v1 on v0

v1 whole, which is shorter than its diff:
```python
import functools

import jax
import jax.numpy as jnp
from jax import lax
from jax.experimental import pallas as pl
from jax.experimental.pallas import tpu as pltpu
from jax.sharding import PartitionSpec as P

MESH = pl.DeviceIdType.MESH
SLOTS = 4


def kernel(n, a_hbm, g_hbm, out_hbm, a_v, g_v, part, held, done, a_sem, g_sem, send_sem, recv_sem, out_sem):
    matrices, halves, _, rows, cols = held.shape
    me = lax.axis_index("dp")
    peers = (lax.rem(me + 1, n), lax.rem(me + n - 1, n))

    def block(h, s):
        return lax.rem(me + n + n - 1 - s, n) if h == 0 else lax.rem(me + 1 + s, n)

    def load_a(m, h):
        return pltpu.make_async_copy(a_hbm.at[0, m, :, pl.ds(h * rows, rows)], a_v.at[m, h], a_sem.at[m, h])

    def load_g(i, h):
        b = pl.multiple_of(block(h, lax.div(i, matrices)) * cols, cols)
        slot = lax.rem(2 * i + h, SLOTS)
        return pltpu.make_async_copy(g_hbm.at[0, lax.rem(i, matrices), :, pl.ds(b, cols)], g_v.at[slot], g_sem.at[slot])

    def hop(buf, phase, m, h, s, b):
        at = ((phase * n + s) * matrices + m) * halves + h
        return pltpu.make_async_remote_copy(
            src_ref=buf.at[m, h, b], dst_ref=buf.at[m, h, b], send_sem=send_sem.at[at], recv_sem=recv_sem.at[at],
            device_id={"dp": peers[h]}, device_id_type=MESH,
        )

    def put(m, h, b):
        return pltpu.make_async_copy(
            done.at[m, h, b],
            out_hbm.at[m, pl.ds(h * rows, rows), pl.ds(pl.multiple_of(b * cols, cols), cols)],
            out_sem.at[(m * halves + h) * n + b],
        )

    items = n * matrices

    def term(i, m, h):
        load_g(i, h).wait()
        part[...] = lax.dot_general(
            a_v[m, h], g_v[lax.rem(2 * i + h, SLOTS)], (((0,), (0,)), ((), ())), preferred_element_type=jnp.float32
        )

        @pl.when(i + SLOTS // 2 < items)
        def _():
            load_g(i + SLOTS // 2, h).start()

    for h in range(halves):
        load_a(0, h).start()
        load_g(0, h).start()
    for h in range(halves):
        load_g(1, h).start()
    barrier = pltpu.get_barrier_semaphore()
    for p in peers:
        pl.semaphore_signal(barrier, inc=1, device_id={"dp": p}, device_id_type=MESH)
    pl.semaphore_wait(barrier, 2)

    def first(m, c):
        for h in range(halves):
            @pl.when(m + 1 < matrices)
            def _():
                load_a(m + 1, h).start()

            load_a(m, h).wait()
            term(m, m, h)
            b = block(h, 0)
            held[m, h, b] = part[...].astype(held.dtype)
            hop(held, 0, m, h, 0, b).start()
        return c

    lax.fori_loop(0, matrices, first, 0)

    def middle(i, c):
        m, s = lax.rem(i, matrices), lax.div(i, matrices)
        for h in range(halves):
            term(i, m, h)
            b = block(h, s)
            hop(held, 0, m, h, s - 1, b).wait_recv()
            held[m, h, b] = (part[...] + held[m, h, b].astype(jnp.float32)).astype(held.dtype)
            hop(held, 0, m, h, s, b).start()
        return c

    lax.fori_loop(matrices, items - matrices, middle, 0)

    def last(m, c):
        i = items - matrices + m
        for h in range(halves):
            term(i, m, h)
            hop(held, 0, m, h, n - 2, me).wait_recv()
            done[m, h, me] = (part[...] + held[m, h, me].astype(jnp.float32)).astype(done.dtype)
            hop(done, 1, m, h, 0, me).start()
            put(m, h, me).start()
        return c

    lax.fori_loop(0, matrices, last, 0)

    def gather(i, c):
        m, s = lax.rem(i, matrices), lax.div(i, matrices) + 1
        for h in range(halves):
            b = lax.rem(me + n - s, n) if h == 0 else lax.rem(me + s, n)
            hop(done, 1, m, h, s - 1, b).wait_recv()

            @pl.when(s < n - 1)
            def _():
                hop(done, 1, m, h, s, b).start()

            put(m, h, b).start()
        return c

    lax.fori_loop(0, items - matrices, gather, 0)

    def drain(i, c):
        m, s = lax.rem(i, matrices), lax.div(i, matrices)
        for h in range(halves):
            hop(held, 0, m, h, s, me).wait_send()
            hop(done, 1, m, h, s, me).wait_send()
            put(m, h, s).wait()
        return c

    lax.fori_loop(0, items - matrices, drain, 0)
    for m in range(matrices):
        for h in range(halves):
            put(m, h, n - 1).wait()


def solution(mesh):
    n = mesh.shape["dp"]

    def step(a, g):
        _, matrices, tokens, d = a.shape
        ff = g.shape[3]
        rows, cols = d // 2, ff // n
        blocks = (matrices, 2, n, rows, cols)
        return pl.pallas_call(
            functools.partial(kernel, n),
            out_shape=jax.ShapeDtypeStruct((matrices, d, ff), jnp.bfloat16),
            in_specs=[pl.BlockSpec(memory_space=pl.ANY)] * 2,
            out_specs=pl.BlockSpec(memory_space=pl.ANY),
            scratch_shapes=[
                pltpu.VMEM((matrices, 2, tokens, rows), jnp.bfloat16),
                pltpu.VMEM((SLOTS, tokens, cols), jnp.bfloat16),
                pltpu.VMEM((rows, cols), jnp.float32),
                pltpu.VMEM(blocks, jnp.bfloat16),
                pltpu.VMEM(blocks, jnp.bfloat16),
                pltpu.SemaphoreType.DMA((matrices, 2)),
                pltpu.SemaphoreType.DMA((SLOTS,)),
                pltpu.SemaphoreType.DMA((2 * n * matrices * 2,)),
                pltpu.SemaphoreType.DMA((2 * n * matrices * 2,)),
                pltpu.SemaphoreType.DMA((matrices * 2 * n,)),
            ],
            compiler_params=pltpu.CompilerParams(
                collective_id=0, has_side_effects=True, vmem_limit_bytes=67043328
            ),
            cost_estimate=pl.CostEstimate(
                flops=2 * matrices * tokens * d * ff, bytes_accessed=2 * matrices * (tokens + d) * (d + ff), transcendentals=0
            ),
        )(a, g)

    return jax.shard_map(
        step, mesh=mesh, in_specs=(P(("rep", "dp")), P(("rep", "dp"))), out_specs=P("rep"), check_vma=False
    )
```

time: 557 us -> 264 us (0.47)
  blocking collectives: 495 us -> 0 us
  Pallas kernels: 0 us -> 253 us
  matrix products: 61.1 us -> 0 us
  local copies, waits for them, and re-layouts: 0 us -> 10.7 us
    dot_general x1 -> x0, blocking collectives: 495 us -> none  [step(): jnp.einsum('rsntd,rsntf->rndf', a, g, preferred_element_type=jnp.float32)]
    pallas_call x0 -> x1, Pallas kernels: none -> 253 us  [step(): pl.pallas_call(functools.partial(kernel, n), out_shape=jax.ShapeDtypeStru...]
    dot_general x1 -> x0, matrix products: 61.1 us -> none  [step(): jnp.einsum('rsntd,rsntf->rndf', a, g, preferred_element_type=jnp.float32)]
    unnamed x0 -> x1, local copies, waits for them, and re-layouts: none -> 10.7 us
where the time goes in v1:
time: 264 us
  Pallas kernels  253 us (96%)
  local copies, waits for them, and re-layouts  10.7 us (4%)
    pallas_call x1, Pallas kernels, step(): pl.pallas_call(functools.partial(kernel, n), out_shape=jax.ShapeDtypeStru...  253 us
    unnamed x1, local copies, waits for them, and re-layouts  10.7 us

profile of v1, /device:TPU:21, one launch (start us, length us, event | category | flops | bytes accessed | tf_op | source)
XLA Modules:
  0.0 264.2 jit_solution(6004207792623314363)
XLA Ops:
  0.0 253.4 %shard_map.28 = bf16[4,768,2048]{2,1,0:T(8,128)(2,1)} custom-call(bf16[1,4,4096,768]{3,2,1,0:T(8,128)(2,1)} %a_hbm.1, bf16[1,4,4096,2048]{3,2,1,0:T(8,128)(2,1)} %g_hbm.1), custom_call_target="tpu_custom_call" | custom-call | flops 51539607552 | bytes 109576192 | tf_op jit(solution)/shard_map/pallas_call | solution.py:142
  253.4 10.7 %copy.4 = bf16[4,768,2048]{2,1,0:T(8,128)(2,1)} copy(bf16[4,768,2048]{2,1,0:T(8,128)(2,1)} %shard_map.28) | data formatting | bytes 25165824

commit v2 on v0

v2 whole, which is shorter than its diff:
```python
import functools

import jax
import jax.numpy as jnp
from jax import lax
from jax.experimental import pallas as pl
from jax.experimental.pallas import tpu as pltpu
from jax.sharding import PartitionSpec as P

MESH = pl.DeviceIdType.MESH
RINGS = 2
SLOTS = 4
STRIPS = ((0, 128), (128, 256), (384, 384))


def kernel(n, a_hbm, g_hbm, out, a_v, g_v, part, held, a_sem, g_sem, send_sem, recv_sem):
    matrices, _, rows, cols = held.shape
    me = lax.axis_index("dp")
    items = n * matrices

    def way(m):
        return 2 * lax.rem(m, RINGS) - 1

    def block(m, s):
        return lax.rem(me + 2 * n + way(m) * (1 + s), n)

    def tile(b):
        return pl.ds(pl.multiple_of(b * cols, cols), cols)

    def load_a(m, k):
        strip = pl.ds(*STRIPS[k])
        return pltpu.make_async_copy(
            a_hbm.at[0, m, :, strip], a_v.at[m, :, strip], a_sem.at[m * len(STRIPS) + k]
        )

    def load_g(i):
        m, slot = lax.rem(i, matrices), lax.rem(i, SLOTS)
        return pltpu.make_async_copy(g_hbm.at[0, m, :, tile(block(m, lax.div(i, matrices)))], g_v.at[slot], g_sem.at[slot])

    def dot(a, i):
        return lax.dot_general(
            a, g_v[lax.rem(i, SLOTS)], (((0,), (0,)), ((), ())), preferred_element_type=jnp.float32
        )

    def hop(phase, m, s, b, strip=None):
        at = (phase * n + s) * matrices + m
        if phase:
            ref = out.at[m, :, tile(b)]
        else:
            ref = held.at[m, b] if strip is None else held.at[m, b, pl.ds(*strip)]
        return pltpu.make_async_remote_copy(
            src_ref=ref, dst_ref=ref, send_sem=send_sem.at[at], recv_sem=recv_sem.at[at],
            device_id={"dp": lax.rem(me + n - way(m), n)}, device_id_type=MESH,
        )

    load_g(0).start()
    load_a(0, 0).start()
    barrier = pltpu.get_barrier_semaphore()
    for m in range(RINGS):
        pl.semaphore_signal(barrier, inc=1, device_id={"dp": lax.rem(me + n - way(m), n)}, device_id_type=MESH)
    load_a(0, 0).wait()
    load_g(1).start()
    load_a(1, 0).start()
    load_g(0).wait()
    for k in range(len(STRIPS)):
        strip = STRIPS[k]
        for m in range(RINGS):
            if m == 1 and k == 0:
                load_g(1).wait()
            if k or m:
                load_a(m, k).wait()
            if k + 1 < len(STRIPS):
                load_a(m, k + 1).start()
            else:
                load_g(RINGS + m).start()
                for j in range(len(STRIPS)):
                    load_a(RINGS + m, j).start()
            b = block(m, 0)
            held[m, b, strip[0] : strip[0] + strip[1]] = dot(a_v[m, :, strip[0] : strip[0] + strip[1]], m).astype(held.dtype)
            if m == 0 and k == 0:
                pl.semaphore_wait(barrier, RINGS)
            hop(0, m, 0, b, strip).start()

    def ahead(i):
        @pl.when(i + SLOTS < items)
        def _():
            load_g(i + SLOTS).start()

    ahead(0)
    ahead(1)

    def first(m, c):
        for k in range(len(STRIPS)):
            load_a(m, k).wait()
        load_g(m).wait()
        b = block(m, 0)
        held[m, b] = dot(a_v[m], m).astype(held.dtype)
        hop(0, m, 0, b).start()
        ahead(m)
        return c

    lax.fori_loop(RINGS, matrices, first, 0)

    def term(i):
        load_g(i).wait()
        part[...] = dot(a_v[lax.rem(i, matrices)], i)
        ahead(i)

    def middle(i, c):
        m, s = lax.rem(i, matrices), lax.div(i, matrices)
        term(i)
        b = block(m, s)
        hop(0, m, s - 1, b).wait_recv()
        held[m, b] = (part[...] + held[m, b].astype(jnp.float32)).astype(held.dtype)
        hop(0, m, s, b).start()
        return c

    lax.fori_loop(matrices, items - matrices, middle, 0)

    def last(m, c):
        term(items - matrices + m)
        hop(0, m, n - 2, me).wait_recv()
        out[m, :, tile(me)] = (part[...] + held[m, me].astype(jnp.float32)).astype(out.dtype)
        hop(1, m, 0, me).start()
        return c

    lax.fori_loop(0, matrices, last, 0)

    def gather(i, c):
        m, s = lax.rem(i, matrices), lax.div(i, matrices) + 1
        b = lax.rem(me + n + way(m) * s, n)
        hop(1, m, s - 1, b).wait_recv()

        @pl.when(s < n - 1)
        def _():
            hop(1, m, s, b).start()

        hop(0, m, s - 1, me).wait_send()
        hop(1, m, s - 1, me).wait_send()
        return c

    lax.fori_loop(0, items - matrices, gather, 0)


def write_out(src, dst, sem):
    copies = [pltpu.make_async_copy(src.at[m], dst.at[m], sem.at[m]) for m in range(src.shape[0])]
    for c in copies:
        c.start()
    for c in copies:
        c.wait()


def solution(mesh):
    n = mesh.shape["dp"]

    def step(a, g):
        _, matrices, tokens, d = a.shape
        ff = g.shape[3]
        cols = ff // n
        hops = 2 * n * matrices
        sums = pl.pallas_call(
            functools.partial(kernel, n),
            out_shape=pltpu.VMEM((matrices, d, ff), jnp.bfloat16),
            in_specs=[pl.BlockSpec(memory_space=pl.ANY)] * 2,
            out_specs=pl.BlockSpec(memory_space=pltpu.VMEM),
            scratch_shapes=[
                pltpu.VMEM((matrices, tokens, d), jnp.bfloat16),
                pltpu.VMEM((SLOTS, tokens, cols), jnp.bfloat16),
                pltpu.VMEM((d, cols), jnp.float32),
                pltpu.VMEM((matrices, n, d, cols), jnp.bfloat16),
                pltpu.SemaphoreType.DMA((matrices * len(STRIPS),)),
                pltpu.SemaphoreType.DMA((SLOTS,)),
                pltpu.SemaphoreType.DMA((hops,)),
                pltpu.SemaphoreType.DMA((hops,)),
            ],
            compiler_params=pltpu.CompilerParams(
                collective_id=0, has_side_effects=True, vmem_limit_bytes=49 << 20
            ),
            cost_estimate=pl.CostEstimate(
                flops=2 * matrices * tokens * d * ff, bytes_accessed=2 * matrices * (tokens + d) * (d + ff), transcendentals=0
            ),
        )(a, g)
        return pl.pallas_call(
            write_out,
            out_shape=jax.ShapeDtypeStruct((matrices, d, ff), jnp.bfloat16),
            in_specs=[pl.BlockSpec(memory_space=pltpu.VMEM)],
            out_specs=pl.BlockSpec(memory_space=pl.ANY),
            scratch_shapes=[pltpu.SemaphoreType.DMA((matrices,))],
            compiler_params=pltpu.CompilerParams(has_side_effects=True, vmem_limit_bytes=1 << 20),
        )(sums)

    return jax.shard_map(
        step, mesh=mesh, in_specs=(P(("rep", "dp")), P(("rep", "dp"))), out_specs=P("rep"), check_vma=False
    )
```

time: 557 us -> 255 us (0.46)
  blocking collectives: 495 us -> 0 us
  Pallas kernels: 0 us -> 255 us
  matrix products: 61.1 us -> 0 us
    dot_general x1 -> x0, blocking collectives: 495 us -> none  [step(): jnp.einsum('rsntd,rsntf->rndf', a, g, preferred_element_type=jnp.float32)]
    pallas_call x0 -> x2, Pallas kernels: none -> 255 us  [the longest x1 250 us: step(): pl.pallas_call(functools.partial(kernel, n), out_shape=pltpu.VMEM((matric...]
    dot_general x1 -> x0, matrix products: 61.1 us -> none  [step(): jnp.einsum('rsntd,rsntf->rndf', a, g, preferred_element_type=jnp.float32)]
where the time goes in v2:
time: 255 us
  Pallas kernels  255 us (100%)
    pallas_call x1, Pallas kernels, step(): pl.pallas_call(functools.partial(kernel, n), out_shape=pltpu.VMEM((matric...  250 us

profile of v2, /device:TPU:21, one launch (start us, length us, event | category | flops | bytes accessed | tf_op | source)
XLA Modules:
  0.0 255.0 jit_solution(9633621813244296803)
XLA Ops:
  0.0 250.3 %shard_map.28.src = bf16[4,768,2048]{2,1,0:T(8,128)(2,1)S(1)} custom-call(bf16[1,4,4096,768]{3,2,1,0:T(8,128)(2,1)} %a_hbm.1, bf16[1,4,4096,2048]{3,2,1,0:T(8,128)(2,1)} %g_hbm.1), custom_call_target="tpu_custom_call" | custom-call | flops 51539607552 | bytes 109576192 | tf_op jit(solution)/shard_map/pallas_call | solution.py:161
  250.3 4.7 %shard_map.29 = bf16[4,768,2048]{2,1,0:T(8,128)(2,1)} custom-call(bf16[4,768,2048]{2,1,0:T(8,128)(2,1)S(1)} %shard_map.28.src), custom_call_target="tpu_custom_call" | custom-call | tf_op jit(solution)/shard_map/pallas_call | solution.py:183

commit v3 on v0

v3 whole, which is shorter than its diff:
```python
import functools

import jax
import jax.numpy as jnp
from jax import lax
from jax.experimental import pallas as pl
from jax.experimental.pallas import tpu as pltpu
from jax.sharding import PartitionSpec as P

MESH = pl.DeviceIdType.MESH
HALVES = 2
SLOTS = 4
STRIP = 128


def kernel(n, a_hbm, g_hbm, out, a_v, g_v, part, held, a_sem, g_sem, send_sem, recv_sem):
    matrices, _, _, rows, cols = held.shape
    me = lax.axis_index("dp")
    peers = (lax.rem(me + 1, n), lax.rem(me + n - 1, n))
    items = n * matrices
    strips = ((0, STRIP), (2 * rows - STRIP, STRIP), (STRIP, 2 * (rows - STRIP)))

    def block(h, s):
        return lax.rem(me + n + n - 1 - s, n) if h == 0 else lax.rem(me + 1 + s, n)

    def tile(h, b):
        return pl.ds(pl.multiple_of((b if h == 0 else lax.rem(b + n - 2, n)) * cols, cols), cols)

    def load_a(m, k=None):
        if k is None:
            return pltpu.make_async_copy(a_hbm.at[0, m], a_v.at[m], a_sem.at[m])
        strip = pl.ds(*strips[k])
        return pltpu.make_async_copy(a_hbm.at[0, m, :, strip], a_v.at[m, :, strip], a_sem.at[k if k == 0 else matrices + k - 1])

    def load_g(i, h):
        slot = lax.rem(2 * i + h, SLOTS)
        return pltpu.make_async_copy(
            g_hbm.at[0, lax.rem(i, matrices), :, tile(h, block(h, lax.div(i, matrices)))], g_v.at[slot], g_sem.at[slot]
        )

    def dot(m, first, size, i, h):
        return lax.dot_general(
            a_v[m, :, first : first + size],
            g_v[lax.rem(2 * i + h, SLOTS)],
            (((0,), (0,)), ((), ())),
            preferred_element_type=jnp.float32,
        )

    def hop(phase, m, h, s, b, strip=None):
        ring = m * HALVES + h
        at = ring * n + lax.rem(s + phase * (n - 1), n)
        if phase:
            ref = out.at[m, pl.ds(h * rows, rows), tile(h, b)]
        else:
            ref = held.at[m, h, b] if strip is None else held.at[m, h, b, pl.ds(*strip)]
        return pltpu.make_async_remote_copy(
            src_ref=ref, dst_ref=ref, send_sem=send_sem.at[ring * 2 + lax.rem(s + phase * (n - 1), 2)], recv_sem=recv_sem.at[at],
            device_id={"dp": peers[h]}, device_id_type=MESH,
        )

    load_g(0, 0).start()
    load_a(0, 0).start()
    load_a(0, 1).start()
    barrier = pltpu.get_barrier_semaphore()
    for p in peers:
        pl.semaphore_signal(barrier, inc=1, device_id={"dp": p}, device_id_type=MESH)
    load_a(0, 0).wait()
    load_a(0, 2).start()
    load_g(0, 0).wait()
    load_g(1, 0).start()
    load_a(1).start()
    for h in range(HALVES):
        b = block(h, 0)
        edge = (0, STRIP) if h == 0 else (rows - STRIP, STRIP)
        if h:
            load_a(0, 1).wait()
        held[0, h, b, edge[0] : edge[0] + STRIP] = dot(0, strips[h][0], STRIP, 0, 0).astype(held.dtype)
        if h == 0:
            pl.semaphore_wait(barrier, len(peers))
        hop(0, 0, h, 0, b, edge).start()
    load_a(0, 2).wait()
    rest = rows - STRIP
    both = dot(0, STRIP, 2 * rest, 0, 0).astype(held.dtype)
    for h in range(HALVES):
        b = block(h, 0)
        edge = (STRIP, rest) if h == 0 else (0, rest)
        held[0, h, b, edge[0] : edge[0] + rest] = both[h * rest : (h + 1) * rest]
        hop(0, 0, h, 0, b, edge).start()

    def first(m, c):
        @pl.when(m + 1 < matrices)
        def _():
            load_g(m + 1, 0).start()
            load_a(m + 1).start()

        load_g(m, 0).wait()
        load_a(m).wait()
        both = dot(m, 0, 2 * rows, m, 0).astype(held.dtype)
        for h in range(HALVES):
            b = block(h, 0)
            held[m, h, b] = both[h * rows : (h + 1) * rows]
            hop(0, m, h, 0, b).start()

        @pl.when(m + 2 >= matrices)
        def _():
            for h in range(HALVES):
                load_g(m + 2, h).start()

        return c

    lax.fori_loop(1, matrices, first, 0)

    def term(i, m, h):
        load_g(i, h).wait()
        part[...] = dot(m, h * rows, rows, i, h)

        @pl.when(i + SLOTS // HALVES < items)
        def _():
            load_g(i + SLOTS // HALVES, h).start()

    def middle(i, c):
        m, s = lax.rem(i, matrices), lax.div(i, matrices)
        for h in range(HALVES):
            term(i, m, h)
            b = block(h, s)
            hop(0, m, h, s - 1, b).wait_recv()
            held[m, h, b] = (part[...] + held[m, h, b].astype(jnp.float32)).astype(held.dtype)

            @pl.when(s >= 2)
            def _():
                hop(0, m, h, s - 2, b).wait_send()

            hop(0, m, h, s, b).start()
        return c

    lax.fori_loop(matrices, items - matrices, middle, 0)

    def last(m, c):
        for h in range(HALVES):
            term(items - matrices + m, m, h)
            hop(0, m, h, n - 2, me).wait_recv()
            out[m, pl.ds(h * rows, rows), tile(h, me)] = (
                part[...] + held[m, h, me].astype(jnp.float32)
            ).astype(out.dtype)
            hop(0, m, h, n - 3, me).wait_send()
            hop(1, m, h, 0, me).start()
        return c

    lax.fori_loop(0, matrices, last, 0)

    def gather(i, c):
        m, s = lax.rem(i, matrices), lax.div(i, matrices) + 1
        for h in range(HALVES):
            b = lax.rem(me + n - s, n) if h == 0 else lax.rem(me + s, n)
            hop(1, m, h, s - 1, b).wait_recv()
            hop(1, m, h, s, b).wait_send()
            hop(1, m, h, s, b).start()
        return c

    lax.fori_loop(0, items - 2 * matrices, gather, 0)

    def end(m, c):
        for h in range(HALVES):
            hop(1, m, h, n - 2, lax.rem(me + 1, n) if h == 0 else lax.rem(me + n - 1, n)).wait_recv()
            for s in range(n - 3, n - 1):
                hop(1, m, h, s, me).wait_send()
        return c

    lax.fori_loop(0, matrices, end, 0)


def write_out(src, dst, sem):
    copies = [pltpu.make_async_copy(src.at[m], dst.at[m], sem.at[m]) for m in range(src.shape[0])]
    for c in copies:
        c.start()
    for c in copies:
        c.wait()


def solution(mesh):
    n = mesh.shape["dp"]

    def step(a, g):
        _, matrices, tokens, d = a.shape
        ff = g.shape[3]
        rows, cols = d // HALVES, ff // n
        rings = matrices * HALVES
        sums = pl.pallas_call(
            functools.partial(kernel, n),
            out_shape=pltpu.VMEM((matrices, d, ff), jnp.bfloat16),
            in_specs=[pl.BlockSpec(memory_space=pl.ANY)] * 2,
            out_specs=pl.BlockSpec(memory_space=pltpu.VMEM),
            scratch_shapes=[
                pltpu.VMEM((matrices, tokens, d), jnp.bfloat16),
                pltpu.VMEM((SLOTS, tokens, cols), jnp.bfloat16),
                pltpu.VMEM((rows, cols), jnp.float32),
                pltpu.VMEM((matrices, HALVES, n, rows, cols), jnp.bfloat16),
                pltpu.SemaphoreType.DMA((matrices + 2,)),
                pltpu.SemaphoreType.DMA((SLOTS,)),
                pltpu.SemaphoreType.DMA((rings * 2,)),
                pltpu.SemaphoreType.DMA((rings * n,)),
            ],
            compiler_params=pltpu.CompilerParams(
                collective_id=0, has_side_effects=True, vmem_limit_bytes=49 << 20
            ),
            cost_estimate=pl.CostEstimate(
                flops=2 * matrices * tokens * d * ff, bytes_accessed=2 * matrices * (tokens + d) * (d + ff), transcendentals=0
            ),
        )(a, g)
        return pl.pallas_call(
            write_out,
            out_shape=jax.ShapeDtypeStruct((matrices, d, ff), jnp.bfloat16),
            in_specs=[pl.BlockSpec(memory_space=pltpu.VMEM)],
            out_specs=pl.BlockSpec(memory_space=pl.ANY),
            scratch_shapes=[pltpu.SemaphoreType.DMA((matrices,))],
            compiler_params=pltpu.CompilerParams(has_side_effects=True, vmem_limit_bytes=1 << 20),
        )(sums)

    return jax.shard_map(
        step, mesh=mesh, in_specs=(P(("rep", "dp")), P(("rep", "dp"))), out_specs=P("rep"), check_vma=False
    )
```

time: 557 us -> 254 us (0.46)
  blocking collectives: 495 us -> 0 us
  Pallas kernels: 0 us -> 253 us
  matrix products: 61.1 us -> 0 us
    dot_general x1 -> x0, blocking collectives: 495 us -> none  [step(): jnp.einsum('rsntd,rsntf->rndf', a, g, preferred_element_type=jnp.float32)]
    pallas_call x0 -> x2, Pallas kernels: none -> 253 us  [the longest x1 249 us: step(): pl.pallas_call(functools.partial(kernel, n), out_shape=pltpu.VMEM((matric...]
    dot_general x1 -> x0, matrix products: 61.1 us -> none  [step(): jnp.einsum('rsntd,rsntf->rndf', a, g, preferred_element_type=jnp.float32)]
where the time goes in v3:
time: 254 us; the launch traced here: 253 us
  Pallas kernels  253 us (100%)
    pallas_call x1, Pallas kernels, step(): pl.pallas_call(functools.partial(kernel, n), out_shape=pltpu.VMEM((matric...  249 us

profile of v3, /device:TPU:21, one launch (start us, length us, event | category | flops | bytes accessed | tf_op | source)
XLA Modules:
  0.0 253.4 jit_solution(13746322365496817973)
XLA Ops:
  0.0 248.7 %shard_map.28.src = bf16[4,768,2048]{2,1,0:T(8,128)(2,1)S(1)} custom-call(bf16[1,4,4096,768]{3,2,1,0:T(8,128)(2,1)} %a_hbm.1, bf16[1,4,4096,2048]{3,2,1,0:T(8,128)(2,1)} %g_hbm.1), custom_call_target="tpu_custom_call" | custom-call | flops 51539607552 | bytes 109576192 | tf_op jit(solution)/shard_map/pallas_call | solution.py:188
  248.7 4.7 %shard_map.29 = bf16[4,768,2048]{2,1,0:T(8,128)(2,1)} custom-call(bf16[4,768,2048]{2,1,0:T(8,128)(2,1)S(1)} %shard_map.28.src), custom_call_target="tpu_custom_call" | custom-call | tf_op jit(solution)/shard_map/pallas_call | solution.py:210

commit v4 on v3

--- a/solution.py
+++ b/solution.py
@@ -10,6 +10,7 @@
 MESH = pl.DeviceIdType.MESH
 HALVES = 2
 SLOTS = 4
+TURNS = 3
 STRIP = 128
 
 
@@ -47,14 +48,13 @@
         )
 
     def hop(phase, m, h, s, b, strip=None):
-        ring = m * HALVES + h
-        at = ring * n + lax.rem(s + phase * (n - 1), n)
+        ring, u = m * HALVES + h, s + phase * (n - 1)
         if phase:
             ref = out.at[m, pl.ds(h * rows, rows), tile(h, b)]
         else:
             ref = held.at[m, h, b] if strip is None else held.at[m, h, b, pl.ds(*strip)]
         return pltpu.make_async_remote_copy(
-            src_ref=ref, dst_ref=ref, send_sem=send_sem.at[ring * 2 + lax.rem(s + phase * (n - 1), 2)], recv_sem=recv_sem.at[at],
+            src_ref=ref, dst_ref=ref, send_sem=send_sem.at[ring], recv_sem=recv_sem.at[ring * TURNS + lax.rem(u, TURNS)],
             device_id={"dp": peers[h]}, device_id_type=MESH,
         )
 
@@ -125,11 +125,7 @@
             b = block(h, s)
             hop(0, m, h, s - 1, b).wait_recv()
             held[m, h, b] = (part[...] + held[m, h, b].astype(jnp.float32)).astype(held.dtype)
-
-            @pl.when(s >= 2)
-            def _():
-                hop(0, m, h, s - 2, b).wait_send()
-
+            hop(0, m, h, s - 1, b).wait_send()
             hop(0, m, h, s, b).start()
         return c
 
@@ -142,7 +138,7 @@
             out[m, pl.ds(h * rows, rows), tile(h, me)] = (
                 part[...] + held[m, h, me].astype(jnp.float32)
             ).astype(out.dtype)
-            hop(0, m, h, n - 3, me).wait_send()
+            hop(0, m, h, n - 2, me).wait_send()
             hop(1, m, h, 0, me).start()
         return c
 
@@ -153,7 +149,7 @@
         for h in range(HALVES):
             b = lax.rem(me + n - s, n) if h == 0 else lax.rem(me + s, n)
             hop(1, m, h, s - 1, b).wait_recv()
-            hop(1, m, h, s, b).wait_send()
+            hop(1, m, h, s - 1, b).wait_send()
             hop(1, m, h, s, b).start()
         return c
 
@@ -162,8 +158,7 @@
     def end(m, c):
         for h in range(HALVES):
             hop(1, m, h, n - 2, lax.rem(me + 1, n) if h == 0 else lax.rem(me + n - 1, n)).wait_recv()
-            for s in range(n - 3, n - 1):
-                hop(1, m, h, s, me).wait_send()
+            hop(1, m, h, n - 2, me).wait_send()
         return c
 
     lax.fori_loop(0, matrices, end, 0)
@@ -197,8 +192,8 @@
                 pltpu.VMEM((matrices, HALVES, n, rows, cols), jnp.bfloat16),
                 pltpu.SemaphoreType.DMA((matrices + 2,)),
                 pltpu.SemaphoreType.DMA((SLOTS,)),
-                pltpu.SemaphoreType.DMA((rings * 2,)),
-                pltpu.SemaphoreType.DMA((rings * n,)),
+                pltpu.SemaphoreType.DMA((rings,)),
+                pltpu.SemaphoreType.DMA((rings * TURNS,)),
             ],
             compiler_params=pltpu.CompilerParams(
                 collective_id=0, has_side_effects=True, vmem_limit_bytes=49 << 20

time: 254 us -> 253 us (level)
  no operation moved by 1% of the time
where the time goes in v4:
time: 253 us
  Pallas kernels  253 us (100%)
    pallas_call x1, Pallas kernels, step(): pl.pallas_call(functools.partial(kernel, n), out_shape=pltpu.VMEM((matric...  248 us

profile of v4, /device:TPU:21, one launch (start us, length us, event | category | flops | bytes accessed | tf_op | source)
XLA Modules:
  0.0 253.0 jit_solution(4274121675517926010)
XLA Ops:
  0.0 248.3 %shard_map.28.src = bf16[4,768,2048]{2,1,0:T(8,128)(2,1)S(1)} custom-call(bf16[1,4,4096,768]{3,2,1,0:T(8,128)(2,1)} %a_hbm.1, bf16[1,4,4096,2048]{3,2,1,0:T(8,128)(2,1)} %g_hbm.1), custom_call_target="tpu_custom_call" | custom-call | flops 51539607552 | bytes 109576192 | tf_op jit(solution)/shard_map/pallas_call | solution.py:183
  248.3 4.7 %shard_map.29 = bf16[4,768,2048]{2,1,0:T(8,128)(2,1)} custom-call(bf16[4,768,2048]{2,1,0:T(8,128)(2,1)S(1)} %shard_map.28.src), custom_call_target="tpu_custom_call" | custom-call | tf_op jit(solution)/shard_map/pallas_call | solution.py:205
